TPU v7x, 32 devices: a whole 2x2x4 slice. The times are simulated.
32 devices in a mesh: grp: 2 (over x), tok: 8 (over z, y), mdl: 2 (over core).
Axes of the slice: x: 2, y: 2, z: 4, core: 2. Of those that a mesh axis runs over, the one named last changes fastest.
Arguments:
- hidden: bfloat16 [1024, 4096], P(('grp', 'tok'), 'mdl'), parts along dimension 0, may hold values from -3 to 3
- queries: bfloat16 [1024, 16, 128], P(('grp', 'tok'), 'mdl'), parts along dimension 0, may hold values from -8 to 8
- cache: bfloat16 [16, 2048, 4, 2, 128], P(('grp', 'tok'), None, 'mdl'), parts along dimension 0, may hold values from -8 to 8
- cache_lengths: int32 [16], P(('grp', 'tok')), parts along dimension 0, may hold values from 128 to 2048, as said below
- wkv: bfloat16 [4096, 4, 2, 128], P('tok', 'mdl'), may hold values from -0.09375 to 0.09375
- wo: bfloat16 [16, 128, 4096], P('mdl', None, 'tok'), may hold values from -0.5 to 0.5
- attn_gain: bfloat16 [4096], replicated, may hold values from 0.5 to 1.5
- moe_gain: bfloat16 [4096], replicated, may hold values from 0.5 to 1.5
- w_gate: bfloat16 [16, 4096, 1792], P(('tok', 'mdl')), may hold values from -0.09375 to 0.09375
- w_up: bfloat16 [16, 4096, 1792], P(('tok', 'mdl')), may hold values from -0.09375 to 0.09375
- w_down: bfloat16 [16, 1792, 4096], P(('tok', 'mdl')), may hold values from -0.0625 to 0.0625
- expert_ids: int32 [1024, 2], P(('grp', 'tok', 'mdl')), parts along dimension 0, may hold values from 0 to 3, all different within a row; in each aligned block of 32 rows (0 to 31, 32 to 63, ...) at most 18 rows name the same one
- gates: float32 [1024, 2], P(('grp', 'tok', 'mdl')), parts along dimension 0, may hold values from 0.1 to 1
Outputs:
- mixed: bfloat16 [1024, 4096], P(('grp', 'tok', 'mdl')), parts along dimension 0
- fresh_key_value: bfloat16 [1024, 4, 2, 128], P(('grp', 'tok'), 'mdl'), parts along dimension 0
There are 2 independent parts, one for each index of `grp`. A program takes and returns all parts, laid end to end along the dimension named above; an argument that names none is the same for every part. Nothing has to cross between parts.
Inputs may be any that keep to these rules, and one draw needn't show every extreme that they name: `expert_ids`: each token names 2 different experts; in aligned blocks of 32 rows no expert is named by more than 18 rows, a bound that some block reaches. `cache_lengths`: some rollout holds exactly 2048 cached positions.
All inputs are finite; a program needn't handle non-finite values.
Results may differ from a plain program's by a relative error of at most 0.007.
Values may be sent and summed in bfloat16 or wider, within the bound.
A program may use at most 128 MiB of HBM per device.

v0:
```python
import math
import jax
import jax.numpy as jnp
from jax import lax
from jax.sharding import PartitionSpec as P

EXPERTS = 4
TOPK = 2
eps_norm = 1e-05
rope_base = 1000000.0
mask_fill = -1e30


def rms_scale(values_in, gain):
    values = values_in.astype(jnp.float32)
    meansq = jnp.mean(values * values, axis=-1, keepdims=True)
    return values * lax.rsqrt(meansq + eps_norm) * gain.astype(jnp.float32)


def rotate(key_rows, positions):
    half_dim = key_rows.shape[-1] // 2
    inverse = jnp.exp(
        jnp.arange(half_dim, dtype=jnp.float32) * (-2.0 * math.log(rope_base) / key_rows.shape[-1])
    )
    angle = positions.astype(jnp.float32)[:, None] * inverse[None, :]
    cosine = jnp.cos(angle)[:, None, :]
    sine_vals = jnp.sin(angle)[:, None, :]
    front_half = key_rows[..., :half_dim]
    back_half = key_rows[..., half_dim:]
    return jnp.concatenate(
        [front_half * cosine - back_half * sine_vals, back_half * cosine + front_half * sine_vals],
        axis=-1,
    )


def score_rows(query_rows, key_rows, scale_factor):
    return (
        lax.dot_general(
            query_rows, key_rows, (((1,), (1,)), ((), ())), preferred_element_type=jnp.float32
        )
        * scale_factor
    )


def head_attention(query_rows, cache_keys, cache_values, length, new_keys, new_values, head_group):
    row_count = query_rows.shape[0]
    block_len = min(512, cache_keys.shape[0])
    scale_factor = 1.0 / math.sqrt(query_rows.shape[1])
    token_of_row = jnp.arange(row_count) // head_group
    block_total = (length + block_len - 1) // block_len

    def block_scores(block_idx):
        row_offset = block_idx * block_len
        block_keys = lax.dynamic_slice_in_dim(cache_keys, row_offset, block_len, 0)
        allowed = row_offset + jnp.arange(block_len) < length
        return (
            jnp.where(
                allowed[None, :], score_rows(query_rows, block_keys, scale_factor), mask_fill
            ),
            allowed,
        )

    new_allowed = jnp.arange(new_keys.shape[0])[None, :] <= token_of_row[:, None]
    new_scores = jnp.where(new_allowed, score_rows(query_rows, new_keys, scale_factor), mask_fill)
    first_max = jnp.max(new_scores, axis=1)
    first_sum = jnp.sum(
        jnp.where(new_allowed, jnp.exp(new_scores - first_max[:, None]), 0.0), axis=1
    )

    def first_pass(block_idx, carry):
        run_max, run_sum = carry
        scores, allowed = block_scores(block_idx)
        next_max = jnp.maximum(run_max, jnp.max(scores, axis=1))
        weights = jnp.where(allowed[None, :], jnp.exp(scores - next_max[:, None]), 0.0)
        return (next_max, run_sum * jnp.exp(run_max - next_max) + jnp.sum(weights, axis=1))

    row_max, row_sum = lax.fori_loop(0, block_total, first_pass, (first_max, first_sum))
    new_probs = (
        jnp.where(new_allowed, jnp.exp(new_scores - row_max[:, None]), 0.0) / row_sum[:, None]
    ).astype(jnp.bfloat16)
    start_total = jnp.dot(new_probs, new_values, preferred_element_type=jnp.float32)

    def second_pass(block_idx, total):
        scores, allowed = block_scores(block_idx)
        probs = (
            jnp.where(allowed[None, :], jnp.exp(scores - row_max[:, None]), 0.0) / row_sum[:, None]
        ).astype(jnp.bfloat16)
        block_values = lax.dynamic_slice_in_dim(cache_values, block_idx * block_len, block_len, 0)
        return total + jnp.dot(probs, block_values, preferred_element_type=jnp.float32)

    total = lax.fori_loop(0, block_total, second_pass, start_total)
    return total.astype(jnp.bfloat16)


def shards(
    hidden,
    queries,
    cache,
    cache_lengths,
    wkv,
    wo,
    attn_gain,
    moe_gain,
    w_gate,
    w_up,
    w_down,
    expert_ids,
    gates,
):
    full_rows = lax.all_gather(hidden, "mdl", axis=1, tiled=True)
    span_len = full_rows.shape[0]
    normalized_input = rms_scale(full_rows, attn_gain).astype(jnp.bfloat16)
    kv_heads = wkv.shape[1]
    head_dim = wkv.shape[3]
    weight_piece = lax.all_gather(wkv, "tok", axis=0, tiled=True)
    key_value_projection = jnp.dot(
        normalized_input,
        weight_piece.reshape(weight_piece.shape[0], -1),
        preferred_element_type=jnp.float32,
    ).reshape(span_len, kv_heads, 2, head_dim)
    length = cache_lengths[0]
    positions = length + jnp.arange(span_len, dtype=jnp.int32)
    fresh_key_value = jnp.stack(
        [rotate(key_value_projection[:, :, 0], positions), key_value_projection[:, :, 1]], axis=2
    ).astype(jnp.bfloat16)
    head_group = queries.shape[1] // kv_heads
    outputs = []
    for head_index in range(kv_heads):
        query_rows = queries[:, head_index * head_group : (head_index + 1) * head_group].reshape(
            span_len * head_group, head_dim
        )
        attended = head_attention(
            query_rows,
            cache[0, :, head_index, 0],
            cache[0, :, head_index, 1],
            length,
            fresh_key_value[:, head_index, 0],
            fresh_key_value[:, head_index, 1],
            head_group,
        )
        outputs.append(attended.reshape(span_len, head_group * head_dim))
    heads_out = jnp.concatenate(outputs, axis=1)
    weight_piece = lax.all_gather(wo, "tok", axis=2, tiled=True)
    attn_out = jnp.dot(
        heads_out,
        weight_piece.reshape(-1, weight_piece.shape[2]),
        preferred_element_type=jnp.float32,
    )
    core_rows = span_len // lax.axis_size("mdl")
    core_start = lax.axis_index("mdl") * core_rows
    summed_heads = lax.psum(attn_out, "mdl")
    attn_rows = lax.dynamic_slice_in_dim(summed_heads, core_start, core_rows, 0)
    resid = (
        lax.dynamic_slice_in_dim(full_rows, core_start, core_rows, 0).astype(jnp.float32)
        + attn_rows
    )
    moe_in = rms_scale(resid, moe_gain).astype(jnp.bfloat16)
    expert_range = jnp.arange(EXPERTS)
    matches = expert_ids[:, :, None] == expert_range[None, None, :]
    chosen = jnp.sum(matches.astype(jnp.int32), axis=1)
    route = jnp.sum(jnp.where(matches, gates[:, :, None], 0.0), axis=1)
    slot_of = jnp.cumsum(chosen, axis=0) - chosen
    capacity = core_rows * TOPK * 9 // (8 * EXPERTS)
    slot_range = jnp.arange(capacity)
    select = (slot_of.T[:, None, :] == slot_range[None, :, None]) & (chosen.T[:, None, :] > 0)
    send_rows = jnp.einsum(
        "eci,id->ecd", select.astype(jnp.bfloat16), moe_in, preferred_element_type=jnp.float32
    ).astype(jnp.bfloat16)
    owners = lax.axis_size("tok") * lax.axis_size("mdl")
    slabs = owners // EXPERTS
    model_width = moe_in.shape[1]
    core_count = lax.axis_size("mdl")
    send_chip = jnp.repeat(send_rows, slabs // core_count, axis=0)
    received = lax.all_to_all(send_chip, "tok", split_axis=0, concat_axis=0, tiled=True)
    chip_count = received.shape[0]
    item_count = received.shape[1]
    both_cores = lax.all_gather(received[:, None], "mdl", axis=1, tiled=True)
    received = both_cores.reshape(-1, item_count, model_width)
    flat_rows = received.reshape(-1, model_width)
    gate_val = jnp.dot(flat_rows, w_gate[0], preferred_element_type=jnp.float32)
    up_val = jnp.dot(flat_rows, w_up[0], preferred_element_type=jnp.float32)
    slab_hidden = (jax.nn.silu(gate_val) * up_val).astype(jnp.bfloat16)
    slab_out = jnp.dot(slab_hidden, w_down[0], preferred_element_type=jnp.float32).astype(
        jnp.bfloat16
    )
    slab_out = slab_out.reshape(received.shape)
    per_core = slab_out.reshape(chip_count, core_count, item_count, model_width).astype(jnp.float32)
    chip_total = lax.psum_scatter(
        per_core.astype(jnp.bfloat16), "mdl", scatter_dimension=1, tiled=True
    ).astype(jnp.float32)
    returned = lax.all_to_all(
        chip_total[:, 0].astype(jnp.bfloat16), "tok", split_axis=0, concat_axis=0, tiled=True
    ).astype(jnp.float32)
    summed = jnp.sum(returned.reshape(EXPERTS, slabs // core_count, capacity, model_width), axis=1)
    weight_table = select.astype(jnp.float32) * route.T[:, None, :]
    moe_out = jnp.einsum("eci,ecd->id", weight_table, summed, precision=lax.Precision.HIGHEST)
    mixed = (resid + moe_out).astype(jnp.bfloat16)
    return (mixed, fresh_key_value)


def solution(mesh):
    in_specs = (
        P(("grp", "tok"), "mdl"),
        P(("grp", "tok"), "mdl", None),
        P(("grp", "tok"), None, "mdl", None, None),
        P(("grp", "tok")),
        P("tok", "mdl", None, None),
        P("mdl", None, "tok"),
        P(),
        P(),
        P(("tok", "mdl"), None, None),
        P(("tok", "mdl"), None, None),
        P(("tok", "mdl"), None, None),
        P(("grp", "tok", "mdl"), None),
        P(("grp", "tok", "mdl"), None),
    )
    out_specs = (P(("grp", "tok", "mdl"), None), P(("grp", "tok"), "mdl", None, None))
    return jax.shard_map(shards, mesh=mesh, in_specs=in_specs, out_specs=out_specs, check_vma=False)
```

profile of v0, /device:TPU:0, one launch (start us, length us, event | category | flops | bytes accessed | tf_op | source)
XLA Modules:
  0.0 394.5 jit_solution(5354055071857114779)
XLA Ops:
  7.2 0.7 all-gather.5.cloned.1.call-update
  8.0 0.7 all-gather.7.cloned.1.call-update
  8.7 0.0 all-reduce.2.cloned.1.call-start
  9.4 0.7 convert_element_type.71
  10.1 2.5 all_gather.12
  12.6 0.2 fusion.73
  12.8 0.2 multiply_cosine_fusion
  13.1 3.0 fusion.115
  16.1 0.1 copy_bitcast_fusion.2
  16.2 0.1 copy_bitcast_fusion
  16.4 69.3 %all-gather.5.cloned.1.call-done = bf16[4096,2,2,128]{3,2,1,0:T(2,128)(2,1)} async-done(((bf16[512,2,2,128]{3,2,1,0:T(2,128)(2,1)}), bf16[4096,2,2,128]{3,2,1,0:T(2,128)(2,1)}) %all-gather.5.cloned.1.call-update) | async-done | bytes 4194320 | tf_op jit(solution)/shard_map/all_gather | solution.py:115
  85.7 11.3 %copy.85 = bf16[4096,2,2,128]{0,3,2,1:T(8,128)(2,1)} copy(bf16[4096,2,2,128]{3,2,1,0:T(2,128)(2,1)} %all-gather.5.cloned.1.call-done) | data formatting | bytes 8388608 | tf_op jit(solution)/shard_map/reshape | solution.py:118
  97.0 3.7 fusion.119
  100.6 0.1 subtract_convert_fusion
  100.7 0.1 maximum_bitcast_fusion
  100.8 0.2 fusion.118
  101.0 0.2 fusion.117
  101.2 0.1 select_reduce_fusion.3
  101.2 1.1 while.44
  101.3 0.7 add_compare_fusion.8
  101.9 0.3 fusion.144
  102.2 0.2 select_reduce_fusion.7
  102.4 0.2 fusion.92
  102.6 1.2 while.45
  102.6 0.7 add_compare_fusion.9
  103.3 0.5 fusion.148
  103.9 0.1 reshape.162
  103.9 1.1 while.46
  103.9 0.7 add_compare_fusion.10
  104.6 0.3 fusion.150
  104.9 0.2 select_reduce_fusion.8
  105.1 0.2 fusion.93
  105.3 1.2 while.47
  105.3 0.7 add_compare_fusion.11
  106.0 0.5 fusion.154
  106.5 0.1 reshape.164
  106.6 104.6 %all-gather.7.cloned.1.call-done = bf16[8,128,4096]{2,1,0:T(8,128)(2,1)} async-done(((bf16[8,128,512]{2,1,0:T(8,128)(2,1)}), bf16[8,128,4096]{2,1,0:T(8,128)(2,1)}) %all-gather.7.cloned.1.call-update) | async-done | bytes 8388624 | tf_op jit(solution)/shard_map/all_gather | solution.py:143
  211.2 6.1 %fusion.84 = f32[64,4096]{1,0:T(8,128)} fusion(bf16[1024,4096]{1,0:T(8,128)(2,1)} %bitcast.113, bf16[64,512]{1,0:T(8,128)(2,1)S(1)} %reshape.164, bf16[64,512]{1,0:T(8,128)(2,1)S(1)} %reshape.162), kind=kOutput, calls=%fused_computation.98 | convolution fusion | flops 537133056 | bytes 9568256 | tf_op jit(solution)/shard_map/dot_general | solution.py:144
  217.3 0.0 all-gather.9.cloned.1.call-start
  217.4 0.1 copy.74
  217.5 0.1 reduce_window_sum.11
  217.6 0.1 copy.76
  217.7 17.4 %all-reduce.2.cloned.1.call-done = f32[64,4096]{1,0:T(8,128)} async-done(((f32[64,4096]{1,0:T(8,128)}), f32[64,4096]{1,0:T(8,128)}) %all-reduce.2.cloned.1.call-update) | async-done | bytes 1048592 | tf_op jit(solution)/shard_map/psum | solution.py:151
  235.1 1.2 multiply_reduce_fusion
  236.3 1.5 convolution_convert_fusion
  237.8 0.2 broadcast_in_dim.140
  238.0 43.0 %all_to_all.10 = bf16[8,18,4096]{2,1,0:T(8,128)(2,1)S(1)} all-to-all(bf16[8,18,4096]{2,1,0:T(8,128)(2,1)S(1)} %bitcast.114), channel_id=1, replica_groups=mesh['grp'=2,'tok'=8,'mdl'=2] {'tok'}, dimensions={0} | all-to-all | bytes 2359296 | tf_op jit(solution)/shard_map/all_to_all | solution.py:174
  281.0 1.7 copy.77
  282.7 0.2 reduce-scatter.2.cloned.1.call-start
  282.9 9.9 %all-gather.9.cloned.1.call-done = bf16[8,36,4096]{2,0,1:T(8,128)(2,1)} async-done(((bf16[8,18,4096]{2,0,1:T(8,128)(2,1)}), bf16[8,36,4096]{2,0,1:T(8,128)(2,1)}) %all-gather.9.cloned.1.call-update) | async-done | bytes 2359312 | tf_op jit(solution)/shard_map/all_gather | solution.py:177
  292.8 3.0 copy.78
  295.8 2.1 reshape_reshape.6
  297.9 9.1 %fusion.54 = f32[288,1792]{1,0:T(8,128)S(1)} fusion(bf16[288,4096]{1,0:T(8,128)(2,1)} %reshape_reshape.6, bf16[1,4096,1792]{2,1,0:T(8,128)(2,1)} %param.29), kind=kOutput, calls=%fused_computation.62 | convolution fusion | flops 4227858432 | bytes 19103744 | tf_op jit(solution)/shard_map/dot_general | solution.py:180
  307.1 9.9 %fusion.66 = bf16[288,1792]{1,0:T(8,128)(2,1)S(1)} fusion(bf16[288,4096]{1,0:T(8,128)(2,1)S(1)} %copy-done.4, bf16[1,4096,1792]{2,1,0:T(8,128)(2,1)} %param.30, f32[288,1792]{1,0:T(8,128)S(1)} %fusion.54), kind=kOutput, calls=%fused_computation.73 | convolution fusion | flops 4230955008 | bytes 20135936 | tf_op jit(solution)/shard_map/dot_general | solution.py:181
  317.0 5.7 %fusion.56 = bf16[288,4096]{1,0:T(8,128)(2,1)} fusion(bf16[288,1792]{1,0:T(8,128)(2,1)S(1)} %fusion.66, bf16[1,1792,4096]{2,1,0:T(8,128)(2,1)S(1)} %bitcast.122), kind=kOutput, calls=%fused_computation.64 | convolution fusion | flops 4229038080 | bytes 18071552 | tf_op jit(solution)/shard_map/dot_general | solution.py:183
  322.7 2.7 reshape_reshape.7
  325.5 2.7 copy.79
  328.2 11.4 %reduce-scatter.2.cloned.1.call-done = bf16[8,1,18,4096]{3,0,2,1:T(8,128)(2,1)} async-done(((bf16[8,2,18,4096]{3,0,2,1:T(8,128)(2,1)}), bf16[8,1,18,4096]{3,0,2,1:T(8,128)(2,1)}) %reduce-scatter.2.cloned.1.call-update) | async-done | bytes 1179664 | tf_op jit(solution)/shard_map/reduce_scatter | solution.py:188
  339.6 3.2 copy.80
  342.8 5.9 %all-to-all-start.1 = ((bf16[8,18,4096]{2,1,0:T(8,128)(2,1)}), bf16[8,18,4096]{2,1,0:T(8,128)(2,1)S(1)}, u32[]{:S(2)}, u32[]{:S(2)}) async-start(bf16[8,18,4096]{2,1,0:T(8,128)(2,1)} %copy.80), calls=%async_computation.2 | async-start | bytes 3145728 | tf_op jit(solution)/shard_map/all_to_all | solution.py:191
  348.8 0.7 copy.83
  349.5 36.6 %all-to-all-done.1 = bf16[8,18,4096]{2,1,0:T(8,128)(2,1)S(1)} async-done(((bf16[8,18,4096]{2,1,0:T(8,128)(2,1)}), bf16[8,18,4096]{2,1,0:T(8,128)(2,1)S(1)}, u32[]{:S(2)}, u32[]{:S(2)}) %all-to-all-start.1) | async-done | bytes 1179680 | tf_op jit(solution)/shard_map/all_to_all | solution.py:191
  386.0 0.3 convert_reduce_fusion
  386.3 1.6 fusion.60
  (54 shorter events, 0.4 us)
Async XLA Ops:
  7.2 5.9 %copy-start.5 = (bf16[64,8,128]{2,1,0:T(8,128)(2,1)S(1)}, bf16[64,8,128]{2,1,0:T(8,128)(2,1)}, u32[]{:S(2)}) copy-start(bf16[64,8,128]{2,1,0:T(8,128)(2,1)} %param.22) | copy-start | bytes 393220
  7.2 5.9 %copy-start.2 = (bf16[1,2048,2,2,128]{4,3,2,1,0:T(2,128)(2,1)S(1)}, bf16[1,2048,2,2,128]{4,3,2,1,0:T(2,128)(2,1)}, u32[]{:S(2)}) copy-start(bf16[1,2048,2,2,128]{4,3,2,1,0:T(2,128)(2,1)} %param.23) | copy-start | bytes 6291460
  7.2 78.5 %all-gather.5.cloned.1.call-start = ((), (), s32[]{:S(2)}) async-start(), calls=%async_computation.3 | async-start | bytes 4718592 | tf_op jit(solution)/shard_map/all_gather | solution.py:115
  7.9 203.3 %all-gather.7.cloned.1.call-start = ((), (), s32[]{:S(2)}) async-start(), calls=%async_computation.4 | async-start | bytes 9437184 | tf_op jit(solution)/shard_map/all_gather | solution.py:143
  8.7 226.4 %all-reduce.2.cloned.1.call-start = ((), (), s32[]{:S(2)}) async-start(), calls=%async_computation.5 | async-start | bytes 2097152 | tf_op jit(solution)/shard_map/psum | solution.py:151
  12.6 223.7 %copy-start = (bf16[64,4096]{1,0:T(8,128)(2,1)}, bf16[64,4096]{1,0:T(8,128)(2,1)S(1)}, u32[]{:S(2)}) copy-start(bf16[64,4096]{1,0:T(8,128)(2,1)S(1)} %all_gather.12) | copy-start | bytes 1572868
  211.2 6.2 %copy-start.7 = (s32[32,2]{0,1:T(2,128)S(1)}, s32[32,2]{0,1:T(2,128)}, u32[]{:S(2)}) copy-start(s32[32,2]{0,1:T(2,128)} %param.32) | copy-start | bytes 772
  211.2 6.4 %copy-start.6 = (bf16[4096]{0:T(1024)(128)(2,1)S(1)}, bf16[4096]{0:T(1024)(128)(2,1)}, u32[]{:S(2)}) copy-start(bf16[4096]{0:T(1024)(128)(2,1)} %param.28) | copy-start | bytes 24580
  217.3 75.5 %all-gather.9.cloned.1.call-start = ((), (), s32[]{:S(2)}) async-start(), calls=%async_computation.7 | async-start | bytes 3538944 | tf_op jit(solution)/shard_map/all_gather | solution.py:177
  282.7 57.0 %reduce-scatter.2.cloned.1.call-start = ((), (), s32[]{:S(2)}) async-start(), calls=%async_computation.6 | async-start | bytes 3538944 | tf_op jit(solution)/shard_map/reduce_scatter | solution.py:188
  297.9 9.1 %copy-start.4 = (bf16[288,4096]{1,0:T(8,128)(2,1)S(1)}, bf16[288,4096]{1,0:T(8,128)(2,1)}, u32[]{:S(2)}) copy-start(bf16[288,4096]{1,0:T(8,128)(2,1)} %reshape_reshape.6) | copy-start | bytes 7077892
  297.9 19.0 %slice-start = ((s8[14680064]{0:T(1024)(128)(4,1)}), s8[4194304]{0:T(1024)(128)(4,1)S(1)}, s32[]{:S(2)}) async-start(s8[14680064]{0:T(1024)(128)(4,1)} %bitcast.121), calls=%async_computation.8 | async-start | bytes 8388608
  297.9 19.0 %slice-start.1 = ((s8[14680064]{0:T(1024)(128)(4,1)}), s8[4194304]{0:T(1024)(128)(4,1)S(1)}, s32[]{:S(2)}) async-start(s8[14680064]{0:T(1024)(128)(4,1)} %bitcast.121), calls=%async_computation.9 | async-start | bytes 8388608
  307.1 9.9 %slice-start.2 = ((s8[14680064]{0:T(1024)(128)(4,1)}), s8[4194304]{0:T(1024)(128)(4,1)S(1)}, s32[]{:S(2)}) async-start(s8[14680064]{0:T(1024)(128)(4,1)} %bitcast.121), calls=%async_computation.10 | async-start | bytes 8388608
  307.1 9.9 %slice-start.3 = ((s8[14680064]{0:T(1024)(128)(4,1)}), s8[2097152]{0:T(1024)(128)(4,1)S(1)}, s32[]{:S(2)}) async-start(s8[14680064]{0:T(1024)(128)(4,1)} %bitcast.121), calls=%async_computation.11 | async-start | bytes 4194304
  339.6 9.1 %copy-start.8 = (f32[32,2]{0,1:T(2,128)S(1)}, f32[32,2]{0,1:T(2,128)}, u32[]{:S(2)}) copy-start(f32[32,2]{0,1:T(2,128)} %param.33) | copy-start | bytes 772
  342.8 43.2 %all-to-all-start.1 = ((bf16[8,18,4096]{2,1,0:T(8,128)(2,1)}), bf16[8,18,4096]{2,1,0:T(8,128)(2,1)S(1)}, u32[]{:S(2)}, u32[]{:S(2)}) async-start(bf16[8,18,4096]{2,1,0:T(8,128)(2,1)} %copy.80), calls=%async_computation.2 | async-start | bytes 3145728 | tf_op jit(solution)/shard_map/all_to_all | solution.py:191
  348.7 37.6 %copy-start.1 = (bf16[64,4096]{1,0:T(8,128)(2,1)S(1)}, bf16[64,4096]{1,0:T(8,128)(2,1)}, u32[]{:S(2)}) copy-start(bf16[64,4096]{1,0:T(8,128)(2,1)} %copy-done) | copy-start | bytes 1572868
  348.7 37.6 %copy-start.3 = (f32[64,4096]{1,0:T(8,128)S(1)}, f32[64,4096]{1,0:T(8,128)}, u32[]{:S(2)}) copy-start(f32[64,4096]{1,0:T(8,128)} %all-reduce.2.cloned.1.call-done) | copy-start | bytes 3145732
Sparse Core Ops, SparseCore 0:
  10.1 75.5 all-gather.4
  87.7 123.4 all-gather.6
  217.4 17.5 all-reduce.1
  282.8 9.9 all-gather.8
  328.3 11.2 reduce-scatter.1
where the time goes:
time: 395 us; the launch traced here: 394 us
  waiting for transfers between devices  251 us (64%)
  blocking collectives  45.5 us (12%)
  matrix products  39.9 us (10%)
  local copies, waits for them, and re-layouts  31.2 us (8%)
  between operations  14.8 us (4%)
  starting transfers between devices  6.27 us (2%)
  other arithmetic  5.95 us (2%)
    all_gather x1, waiting for transfers between devices, shards(): weight_piece = lax.all_gather(wo, 'tok', axis=2, tiled=True)  105 us
    all_gather x1, waiting for transfers between devices, shards(): weight_piece = lax.all_gather(wkv, 'tok', axis=0, tiled=True)  69.3 us
    all_to_all x1, blocking collectives, shards(): lax.all_to_all(send_chip, 'tok', split_axis=0, concat_axis=0, tiled=True)  43 us
    all_to_all x1, waiting for transfers between devices, shards(): lax.all_to_all(chip_total[:, 0].astype(jnp.bfloat16), 'tok', split_axis=0...  36.6 us
    psum x1, waiting for transfers between devices, shards(): summed_heads = lax.psum(attn_out, 'mdl')  17.4 us
    reduce_scatter x1, waiting for transfers between devices, shards(): lax.psum_scatter(per_core.astype(jnp.bfloat16), 'mdl', scatter_dimension=...  11.4 us
    reshape x1, local copies, waits for them, and re-layouts, shards(): weight_piece.reshape(weight_piece.shape[0], -1)  11.3 us
    all_gather x1, waiting for transfers between devices, shards(): both_cores = lax.all_gather(received[:, None], 'mdl', axis=1, tiled=True)  9.91 us
  transfers between devices with their start and end apart: 6, of which 6 were waited for; matrix products, arithmetic and copies ran while one was open for 7% of the time, Pallas kernels for 0%

commit v1 on v0

--- a/solution.py
+++ b/solution.py
@@ -9,6 +9,29 @@
 eps_norm = 1e-05
 rope_base = 1000000.0
 mask_fill = -1e30
+
+
+def split_up(shard, dim, length):
+    lengths = shard.shape
+    blocks = shard.reshape(*lengths[:dim], length, lengths[dim] // length, *lengths[dim + 1 :])
+    return jnp.moveaxis(blocks, dim, 0)
+
+
+def joined_along(blocks, dim):
+    blocks = jnp.moveaxis(blocks, 0, dim)
+    lengths = blocks.shape
+    return blocks.reshape(*lengths[:dim], lengths[dim] * lengths[dim + 1], *lengths[dim + 2 :])
+
+
+def rotated_exchange(x, axis, split_dim, concat_dim):
+    size, position = (lax.axis_size(axis), lax.axis_index(axis))
+    pieces = split_up(x, split_dim, size)
+    outs = [pieces[position]]
+    for step in range(1, size):
+        sent = pieces[(position + step) % size]
+        outs.append(lax.ppermute(sent, axis, [(i, (i + step) % size) for i in range(size)]))
+    pieces = jnp.stack(outs)[(position - jnp.arange(size)) % size]
+    return joined_along(pieces, concat_dim)
 
 
 def rms_scale(values_in, gain):
@@ -171,7 +194,7 @@
     model_width = moe_in.shape[1]
     core_count = lax.axis_size("mdl")
     send_chip = jnp.repeat(send_rows, slabs // core_count, axis=0)
-    received = lax.all_to_all(send_chip, "tok", split_axis=0, concat_axis=0, tiled=True)
+    received = rotated_exchange(send_chip, "tok", 0, 0)
     chip_count = received.shape[0]
     item_count = received.shape[1]
     both_cores = lax.all_gather(received[:, None], "mdl", axis=1, tiled=True)

time: 395 us -> 393 us (level)
  blocking collectives: 45.5 us -> 2.51 us
  waiting for transfers between devices: 251 us -> 276 us
  starting transfers between devices: 6.27 us -> 21.3 us
    all_to_all x1 -> x0, blocking collectives: 43 us -> none  [shards(): lax.all_to_all(send_chip, 'tok', split_axis=0, concat_axis=0, tiled=True)]
    ppermute x0 -> x7, starting transfers between devices: none -> 14.9 us  [rotated_exchange(): lax.ppermute(sent, axis, [(i, (i + step) % size) for i in range(size)])]
    ppermute x0 -> x7, waiting for transfers between devices: none -> 13.7 us  [rotated_exchange(): lax.ppermute(sent, axis, [(i, (i + step) % size) for i in range(size)])]
    all_gather x1, waiting for transfers between devices: 9.91 us -> 21.2 us  [shards(): both_cores = lax.all_gather(received[:, None], 'mdl', axis=1, tiled=True)]
  transfers between devices with their start and end apart: 6 -> 13, of which waited for: 6 -> 10; matrix products, arithmetic and copies ran while one was open for 7% -> 7% of each run, Pallas kernels for 0% -> 0%
where the time goes in v1:
time: 393 us
  waiting for transfers between devices  276 us (70%)
  matrix products  40 us (10%)
  local copies, waits for them, and re-layouts  32 us (8%)
  starting transfers between devices  21.3 us (5%)
  between operations  15 us (4%)
  other arithmetic  5.97 us (2%)
    all_gather x1, waiting for transfers between devices, shards(): weight_piece = lax.all_gather(wo, 'tok', axis=2, tiled=True)  105 us
    all_gather x1, waiting for transfers between devices, shards(): weight_piece = lax.all_gather(wkv, 'tok', axis=0, tiled=True)  69.3 us
    all_to_all x1, waiting for transfers between devices, shards(): lax.all_to_all(chip_total[:, 0].astype(jnp.bfloat16), 'tok', split_axis=0...  36.5 us
    all_gather x1, waiting for transfers between devices, shards(): both_cores = lax.all_gather(received[:, None], 'mdl', axis=1, tiled=True)  21.2 us
    psum x1, waiting for transfers between devices, shards(): summed_heads = lax.psum(attn_out, 'mdl')  17.3 us
    ppermute x7, starting transfers between devices, rotated_exchange(): lax.ppermute(sent, axis, [(i, (i + step) % size) for i in range(size)])  14.9 us
    ppermute x7, waiting for transfers between devices, rotated_exchange(): lax.ppermute(sent, axis, [(i, (i + step) % size) for i in range(size)])  13.7 us
    reduce_scatter x1, waiting for transfers between devices, shards(): lax.psum_scatter(per_core.astype(jnp.bfloat16), 'mdl', scatter_dimension=...  11.4 us
  transfers between devices with their start and end apart: 13, of which 10 were waited for; matrix products, arithmetic and copies ran while one was open for 7% of the time, Pallas kernels for 0%

profile of v1, /device:TPU:0, one launch (start us, length us, event | category | flops | bytes accessed | tf_op | source)
XLA Modules:
  0.0 392.5 jit_solution(2663439734765282250)
XLA Ops:
  7.2 0.7 all-gather.5.cloned.1.call-update
  8.0 0.7 all-gather.7.cloned.1.call-update
  9.4 0.7 convert_element_type.71
  10.1 2.5 all_gather.12
  12.6 0.2 fusion.73
  12.8 0.2 multiply_cosine_fusion
  13.1 3.0 fusion.117
  16.2 0.1 copy_bitcast_fusion
  16.4 69.3 %all-gather.5.cloned.1.call-done = bf16[4096,2,2,128]{3,2,1,0:T(2,128)(2,1)} async-done(((bf16[512,2,2,128]{3,2,1,0:T(2,128)(2,1)}), bf16[4096,2,2,128]{3,2,1,0:T(2,128)(2,1)}) %all-gather.5.cloned.1.call-update) | async-done | bytes 4194320 | tf_op jit(solution)/shard_map/all_gather | solution.py:138
  85.7 11.3 %copy.98 = bf16[4096,2,2,128]{0,3,2,1:T(8,128)(2,1)} copy(bf16[4096,2,2,128]{3,2,1,0:T(2,128)(2,1)} %all-gather.5.cloned.1.call-done) | data formatting | bytes 8388608 | tf_op jit(solution)/shard_map/reshape | solution.py:141
  96.9 3.7 fusion.121
  100.8 0.2 fusion.120
  101.0 0.2 fusion.119
  101.2 1.1 while.44
  101.2 0.7 add_compare_fusion.8
  101.9 0.3 fusion.146
  102.2 0.2 select_reduce_fusion.7
  102.4 0.2 fusion.92
  102.6 1.2 while.45
  102.6 0.7 add_compare_fusion.9
  103.3 0.5 fusion.150
  103.9 1.1 while.46
  103.9 0.7 add_compare_fusion.10
  104.6 0.3 fusion.152
  104.9 0.2 select_reduce_fusion.8
  105.1 0.2 fusion.93
  105.3 1.2 while.47
  105.3 0.7 add_compare_fusion.11
  105.9 0.5 fusion.156
  106.6 104.6 %all-gather.7.cloned.1.call-done = bf16[8,128,4096]{2,1,0:T(8,128)(2,1)} async-done(((bf16[8,128,512]{2,1,0:T(8,128)(2,1)}), bf16[8,128,4096]{2,1,0:T(8,128)(2,1)}) %all-gather.7.cloned.1.call-update) | async-done | bytes 8388624 | tf_op jit(solution)/shard_map/all_gather | solution.py:166
  211.2 6.1 %fusion.84 = f32[64,4096]{1,0:T(8,128)} fusion(bf16[1024,4096]{1,0:T(8,128)(2,1)} %bitcast.144, bf16[64,512]{1,0:T(8,128)(2,1)S(1)} %reshape.210, bf16[64,512]{1,0:T(8,128)(2,1)S(1)} %reshape.208), kind=kOutput, calls=%fused_computation.114 | convolution fusion | flops 537133056 | bytes 9568256 | tf_op jit(solution)/shard_map/dot_general | solution.py:167
  217.8 17.3 %all-reduce.2.cloned.1.call-done = f32[64,4096]{1,0:T(8,128)} async-done(((f32[64,4096]{1,0:T(8,128)}), f32[64,4096]{1,0:T(8,128)}) %all-reduce.2.cloned.1.call-update) | async-done | bytes 1048592 | tf_op jit(solution)/shard_map/psum | solution.py:174
  235.1 1.2 multiply_reduce_fusion
  236.3 1.5 convolution_convert_fusion
  237.8 0.2 broadcast_in_dim.138
  238.1 1.8 collective-permute-start
  240.0 1.5 collective-permute-start.1
  241.5 2.4 collective-permute-start.2
  243.9 1.4 collective-permute-start.3
  245.3 2.4 collective-permute-start.4
  247.7 1.1 collective-permute-done
  248.8 1.6 collective-permute-start.5
  250.5 3.7 collective-permute-start.6
  254.2 10.8 %collective-permute-done.2 = bf16[1,18,4096]{2,1,0:T(8,128)(2,1)S(1)} collective-permute-done((bf16[1,18,4096]{2,1,0:T(8,128)(2,1)S(1)}, bf16[1,18,4096]{2,1,0:T(8,128)(2,1)S(1)}, u32[]{:S(2)}, u32[]{:S(2)}) %collective-permute-start.2) | collective-permute-done | bytes 147488 | tf_op jit(solution)/shard_map/ppermute | solution.py:32
  265.0 0.5 collective-permute-done.3
  265.7 1.3 collective-permute-done.6
  266.9 0.6 gather_fusion
  267.6 1.7 copy.90
  269.3 0.2 reduce-scatter.2.cloned.1.call-start
  269.5 21.2 %all-gather.9.cloned.1.call-done = bf16[8,36,4096]{2,0,1:T(8,128)(2,1)} async-done(((bf16[8,18,4096]{2,0,1:T(8,128)(2,1)}), bf16[8,36,4096]{2,0,1:T(8,128)(2,1)}) %all-gather.9.cloned.1.call-update) | async-done | bytes 2359312 | tf_op jit(solution)/shard_map/all_gather | solution.py:200
  290.8 3.0 copy.91
  293.7 2.1 reshape_reshape.10
  295.9 9.1 %fusion.54 = f32[288,1792]{1,0:T(8,128)S(1)} fusion(bf16[288,4096]{1,0:T(8,128)(2,1)} %reshape_reshape.10, bf16[1,4096,1792]{2,1,0:T(8,128)(2,1)} %param.29), kind=kOutput, calls=%fused_computation.63 | convolution fusion | flops 4227858432 | bytes 19103744 | tf_op jit(solution)/shard_map/dot_general | solution.py:203
  305.0 9.9 %fusion.66 = bf16[288,1792]{1,0:T(8,128)(2,1)S(1)} fusion(bf16[288,4096]{1,0:T(8,128)(2,1)S(1)} %copy-done.4, bf16[1,4096,1792]{2,1,0:T(8,128)(2,1)} %param.30, f32[288,1792]{1,0:T(8,128)S(1)} %fusion.54), kind=kOutput, calls=%fused_computation.74 | convolution fusion | flops 4230955008 | bytes 20135936 | tf_op jit(solution)/shard_map/dot_general | solution.py:204
  314.9 5.8 %fusion.56 = bf16[288,4096]{1,0:T(8,128)(2,1)} fusion(bf16[288,1792]{1,0:T(8,128)(2,1)S(1)} %fusion.66, bf16[1,1792,4096]{2,1,0:T(8,128)(2,1)S(1)} %bitcast.154), kind=kOutput, calls=%fused_computation.65 | convolution fusion | flops 4229038080 | bytes 18071552 | tf_op jit(solution)/shard_map/dot_general | solution.py:206
  320.7 2.7 reshape_reshape.11
  323.4 2.7 copy.92
  326.2 11.4 %reduce-scatter.2.cloned.1.call-done = bf16[8,1,18,4096]{3,0,2,1:T(8,128)(2,1)} async-done(((bf16[8,2,18,4096]{3,0,2,1:T(8,128)(2,1)}), bf16[8,1,18,4096]{3,0,2,1:T(8,128)(2,1)}) %reduce-scatter.2.cloned.1.call-update) | async-done | bytes 1179664 | tf_op jit(solution)/shard_map/reduce_scatter | solution.py:211
  337.6 3.1 copy.93
  340.7 6.0 %all-to-all-start = ((bf16[8,18,4096]{2,1,0:T(8,128)(2,1)}), bf16[8,18,4096]{2,1,0:T(8,128)(2,1)S(1)}, u32[]{:S(2)}, u32[]{:S(2)}) async-start(bf16[8,18,4096]{2,1,0:T(8,128)(2,1)} %copy.93), calls=%async_computation.1 | async-start | bytes 3145728 | tf_op jit(solution)/shard_map/all_to_all | solution.py:214
  346.8 0.7 copy.96
  347.5 36.5 %all-to-all-done = bf16[8,18,4096]{2,1,0:T(8,128)(2,1)S(1)} async-done(((bf16[8,18,4096]{2,1,0:T(8,128)(2,1)}), bf16[8,18,4096]{2,1,0:T(8,128)(2,1)S(1)}, u32[]{:S(2)}, u32[]{:S(2)}) %all-to-all-start) | async-done | bytes 1179680 | tf_op jit(solution)/shard_map/all_to_all | solution.py:214
  384.1 0.3 convert_reduce_fusion
  384.4 1.6 fusion.60
  (78 shorter events, 1.4 us)
Async XLA Ops:
  7.2 5.9 %copy-start.5 = (bf16[64,8,128]{2,1,0:T(8,128)(2,1)S(1)}, bf16[64,8,128]{2,1,0:T(8,128)(2,1)}, u32[]{:S(2)}) copy-start(bf16[64,8,128]{2,1,0:T(8,128)(2,1)} %param.22) | copy-start | bytes 393220
  7.2 5.9 %copy-start.2 = (bf16[1,2048,2,2,128]{4,3,2,1,0:T(2,128)(2,1)S(1)}, bf16[1,2048,2,2,128]{4,3,2,1,0:T(2,128)(2,1)}, u32[]{:S(2)}) copy-start(bf16[1,2048,2,2,128]{4,3,2,1,0:T(2,128)(2,1)} %param.23) | copy-start | bytes 6291460
  7.2 78.5 %all-gather.5.cloned.1.call-start = ((), (), s32[]{:S(2)}) async-start(), calls=%async_computation.2 | async-start | bytes 4718592 | tf_op jit(solution)/shard_map/all_gather | solution.py:138
  7.9 203.3 %all-gather.7.cloned.1.call-start = ((), (), s32[]{:S(2)}) async-start(), calls=%async_computation.3 | async-start | bytes 9437184 | tf_op jit(solution)/shard_map/all_gather | solution.py:166
  8.7 226.4 %all-reduce.2.cloned.1.call-start = ((), (), s32[]{:S(2)}) async-start(), calls=%async_computation.4 | async-start | bytes 2097152 | tf_op jit(solution)/shard_map/psum | solution.py:174
  12.6 223.7 %copy-start = (bf16[64,4096]{1,0:T(8,128)(2,1)}, bf16[64,4096]{1,0:T(8,128)(2,1)S(1)}, u32[]{:S(2)}) copy-start(bf16[64,4096]{1,0:T(8,128)(2,1)S(1)} %all_gather.12) | copy-start | bytes 1572868
  211.2 6.3 %copy-start.7 = (s32[32,2]{0,1:T(2,128)S(1)}, s32[32,2]{0,1:T(2,128)}, u32[]{:S(2)}) copy-start(s32[32,2]{0,1:T(2,128)} %param.32) | copy-start | bytes 772
  211.2 6.5 %copy-start.6 = (bf16[4096]{0:T(1024)(128)(2,1)S(1)}, bf16[4096]{0:T(1024)(128)(2,1)}, u32[]{:S(2)}) copy-start(bf16[4096]{0:T(1024)(128)(2,1)} %param.28) | copy-start | bytes 24580
  217.3 73.4 %all-gather.9.cloned.1.call-start = ((), (), s32[]{:S(2)}) async-start(), calls=%async_computation.6 | async-start | bytes 3538944 | tf_op jit(solution)/shard_map/all_gather | solution.py:200
  238.1 10.7 %collective-permute-start = (bf16[1,18,4096]{2,1,0:T(8,128)(2,1)S(1)}, bf16[1,18,4096]{2,1,0:T(8,128)(2,1)S(1)}, u32[]{:S(2)}, u32[]{:S(2)}) collective-permute-start(bf16[1,18,4096]{2,1,0:T(8,128)(2,1)S(1)} %get-tuple-element.274), channel_id=1, source_target_pairs={{0,2},{2,4},{4,6},{6,8},{8,10},{10,12},{12,14},{14,0},{1,3},{3,5},... | collective-permute-start | bytes 442376 | tf_op jit(solution)/shard_map/ppermute | solution.py:32
  240.0 10.5 %collective-permute-start.1 = (bf16[1,18,4096]{2,1,0:T(8,128)(2,1)S(1)}, bf16[1,18,4096]{2,1,0:T(8,128)(2,1)S(1)}, u32[]{:S(2)}, u32[]{:S(2)}) collective-permute-start(bf16[1,18,4096]{2,1,0:T(8,128)(2,1)S(1)} %get-tuple-element.273), channel_id=1, source_target_pairs={{0,4},{2,6},{4,8},{6,10},{8,12},{10,14},{12,0},{14,2},{1,5},{3,7},... | collective-permute-start | bytes 442376 | tf_op jit(solution)/shard_map/ppermute | solution.py:32
  241.5 23.5 %collective-permute-start.2 = (bf16[1,18,4096]{2,1,0:T(8,128)(2,1)S(1)}, bf16[1,18,4096]{2,1,0:T(8,128)(2,1)S(1)}, u32[]{:S(2)}, u32[]{:S(2)}) collective-permute-start(bf16[1,18,4096]{2,1,0:T(8,128)(2,1)S(1)} %get-tuple-element.272), channel_id=1, source_target_pairs={{0,6},{2,8},{4,10},{6,12},{8,14},{10,0},{12,2},{14,4},{1,7},{3,9},... | collective-permute-start | bytes 442376 | tf_op jit(solution)/shard_map/ppermute | solution.py:32
  243.9 21.7 %collective-permute-start.3 = (bf16[1,18,4096]{2,1,0:T(8,128)(2,1)S(1)}, bf16[1,18,4096]{2,1,0:T(8,128)(2,1)S(1)}, u32[]{:S(2)}, u32[]{:S(2)}) collective-permute-start(bf16[1,18,4096]{2,1,0:T(8,128)(2,1)S(1)} %get-tuple-element.271), channel_id=1, source_target_pairs={{0,8},{2,10},{4,12},{6,14},{8,0},{10,2},{12,4},{14,6},{1,9},{3,11}... | collective-permute-start | bytes 442376 | tf_op jit(solution)/shard_map/ppermute | solution.py:32
  245.3 20.3 %collective-permute-start.4 = (bf16[1,18,4096]{2,1,0:T(8,128)(2,1)S(1)}, bf16[1,18,4096]{2,1,0:T(8,128)(2,1)S(1)}, u32[]{:S(2)}, u32[]{:S(2)}) collective-permute-start(bf16[1,18,4096]{2,1,0:T(8,128)(2,1)S(1)} %get-tuple-element.270), channel_id=1, source_target_pairs={{0,10},{2,12},{4,14},{6,0},{8,2},{10,4},{12,6},{14,8},{1,11},{3,13... | collective-permute-start | bytes 442376 | tf_op jit(solution)/shard_map/ppermute | solution.py:32
  248.8 16.8 %collective-permute-start.5 = (bf16[1,18,4096]{2,1,0:T(8,128)(2,1)S(1)}, bf16[1,18,4096]{2,1,0:T(8,128)(2,1)S(1)}, u32[]{:S(2)}, u32[]{:S(2)}) collective-permute-start(bf16[1,18,4096]{2,1,0:T(8,128)(2,1)S(1)} %get-tuple-element.269), channel_id=1, source_target_pairs={{0,12},{2,14},{4,0},{6,2},{8,4},{10,6},{12,8},{14,10},{1,13},{3,15... | collective-permute-start | bytes 442376 | tf_op jit(solution)/shard_map/ppermute | solution.py:32
  250.5 16.4 %collective-permute-start.6 = (bf16[1,18,4096]{2,1,0:T(8,128)(2,1)S(1)}, bf16[1,18,4096]{2,1,0:T(8,128)(2,1)S(1)}, u32[]{:S(2)}, u32[]{:S(2)}) collective-permute-start(bf16[1,18,4096]{2,1,0:T(8,128)(2,1)S(1)} %get-tuple-element.268), channel_id=1, source_target_pairs={{0,14},{2,0},{4,2},{6,4},{8,6},{10,8},{12,10},{14,12},{1,15},{3,1}... | collective-permute-start | bytes 442376 | tf_op jit(solution)/shard_map/ppermute | solution.py:32
  269.3 68.3 %reduce-scatter.2.cloned.1.call-start = ((), (), s32[]{:S(2)}) async-start(), calls=%async_computation.5 | async-start | bytes 3538944 | tf_op jit(solution)/shard_map/reduce_scatter | solution.py:211
  295.9 9.1 %copy-start.4 = (bf16[288,4096]{1,0:T(8,128)(2,1)S(1)}, bf16[288,4096]{1,0:T(8,128)(2,1)}, u32[]{:S(2)}) copy-start(bf16[288,4096]{1,0:T(8,128)(2,1)} %reshape_reshape.10) | copy-start | bytes 7077892
  295.9 19.0 %slice-start = ((s8[14680064]{0:T(1024)(128)(4,1)}), s8[4194304]{0:T(1024)(128)(4,1)S(1)}, s32[]{:S(2)}) async-start(s8[14680064]{0:T(1024)(128)(4,1)} %bitcast.153), calls=%async_computation.7 | async-start | bytes 8388608
  295.9 19.0 %slice-start.1 = ((s8[14680064]{0:T(1024)(128)(4,1)}), s8[4194304]{0:T(1024)(128)(4,1)S(1)}, s32[]{:S(2)}) async-start(s8[14680064]{0:T(1024)(128)(4,1)} %bitcast.153), calls=%async_computation.8 | async-start | bytes 8388608
  305.0 9.9 %slice-start.2 = ((s8[14680064]{0:T(1024)(128)(4,1)}), s8[4194304]{0:T(1024)(128)(4,1)S(1)}, s32[]{:S(2)}) async-start(s8[14680064]{0:T(1024)(128)(4,1)} %bitcast.153), calls=%async_computation.9 | async-start | bytes 8388608
  305.0 9.9 %slice-start.3 = ((s8[14680064]{0:T(1024)(128)(4,1)}), s8[2097152]{0:T(1024)(128)(4,1)S(1)}, s32[]{:S(2)}) async-start(s8[14680064]{0:T(1024)(128)(4,1)} %bitcast.153), calls=%async_computation.10 | async-start | bytes 4194304
  340.7 6.0 %copy-start.8 = (f32[32,2]{0,1:T(2,128)S(1)}, f32[32,2]{0,1:T(2,128)}, u32[]{:S(2)}) copy-start(f32[32,2]{0,1:T(2,128)} %param.33) | copy-start | bytes 772
  340.7 43.3 %all-to-all-start = ((bf16[8,18,4096]{2,1,0:T(8,128)(2,1)}), bf16[8,18,4096]{2,1,0:T(8,128)(2,1)S(1)}, u32[]{:S(2)}, u32[]{:S(2)}) async-start(bf16[8,18,4096]{2,1,0:T(8,128)(2,1)} %copy.93), calls=%async_computation.1 | async-start | bytes 3145728 | tf_op jit(solution)/shard_map/all_to_all | solution.py:214
  346.8 37.6 %copy-start.1 = (bf16[64,4096]{1,0:T(8,128)(2,1)S(1)}, bf16[64,4096]{1,0:T(8,128)(2,1)}, u32[]{:S(2)}) copy-start(bf16[64,4096]{1,0:T(8,128)(2,1)} %copy-done) | copy-start | bytes 1572868
  346.8 37.6 %copy-start.3 = (f32[64,4096]{1,0:T(8,128)S(1)}, f32[64,4096]{1,0:T(8,128)}, u32[]{:S(2)}) copy-start(f32[64,4096]{1,0:T(8,128)} %all-reduce.2.cloned.1.call-done) | copy-start | bytes 3145732
Sparse Core Ops, SparseCore 0:
  10.1 75.5 all-gather.4
  87.7 123.4 all-gather.6
  217.5 17.5 all-reduce.1
  269.4 21.2 all-gather.8
  326.3 11.2 reduce-scatter.1
